TPU v7x, 512 devices: a whole 4x4x16 slice. The times are simulated.
512 devices in a mesh: nodes: 128 (over z, x, core), mp: 4 (over y).
Axes of the slice: x: 4, y: 4, z: 16, core: 2. Of those that a mesh axis runs over, the one named last changes fastest.
Arguments:
- grid_in: bfloat16 [131072, 1024], P('nodes', 'mp'), may hold values from -2200 to 2200
- mesh_in: bfloat16 [32768, 1024], P('nodes', 'mp'), may hold values from -2200 to 2200
- w_query: bfloat16 [4, 1024, 512], P(None, None, 'mp'), as said below
- w_key: bfloat16 [4, 1024, 512], P(None, None, 'mp'), may hold values from -8 to 8
- w_value: bfloat16 [4, 1024, 512], P(None, None, 'mp'), may hold values from -0.1875 to 0.1875
- w_out: bfloat16 [4, 512, 1024], P(None, 'mp'), may hold values from -1 to 1
- norm_gains: float32 [6, 1024], replicated, may hold values from 0.25 to 1.75
- enc_list: int32 [256, 4], P('nodes'), may hold values from 0 to 1023, as said below
- proc_list: int32 [256, 3], P('nodes'), may hold values from 0 to 255, as said below
- dec_list: int32 [1024, 2], P('nodes'), may hold values from 0 to 255, as said below
- grid_count: int32 [1024], replicated, may hold values from 1 to 128
Outputs:
- grid_out: bfloat16 [131072, 1024], P('nodes', 'mp')
- mesh_out: bfloat16 [32768, 1024], P('nodes', 'mp')
Inputs may be any that keep to these rules, and one draw needn't show every extreme that they name: `enc_list`: mesh block b lies with node index b // 2; its 4 entries are distinct grid blocks held by node indices at most 2 from it (grid block c lies with node index c // 8). `proc_list`: entry 0 of row b is b; the others are distinct mesh blocks other than b held by node indices at most 2 from b's. `dec_list`: grid block c's 2 entries are distinct mesh blocks held by node indices at most 2 from c's. `w_query`: entries within 6 / sqrt(1024) of zero.
All inputs are finite; a program needn't handle non-finite values.
Results may differ from a plain program's by a relative error of at most 0.019.
Values may be sent and summed in bfloat16 or wider, within the bound.
No kernel may reach another device: no remote copies, remote signals or barrier semaphores. Data moves between devices by JAX's collectives and lax.ppermute only.
A program may use at most 64 MiB of HBM per device.

v0:
```python
import jax
import jax.numpy as jnp
from jax import lax
from jax.sharding import PartitionSpec as P

HEAD_DIM = 64
BLOCK = 128
REACH = 2
epsilon = 1e-05


def in_blocks(value, dim, count):
    lengths = value.shape
    pieces = value.reshape(*lengths[:dim], count, lengths[dim] // count, *lengths[dim + 1 :])
    return jnp.moveaxis(pieces, dim, 0)


def summed_on_arrival(value, axis, dim):
    pieces = in_blocks(value, dim, lax.axis_size(axis))
    arrived = lax.all_to_all(pieces, axis, split_axis=0, concat_axis=0, tiled=True)
    return arrived.astype(jnp.float32).sum(axis=0)


def from_behind(value, axis, steps):
    count = lax.axis_size(axis)
    first, last = (max(0, -steps), min(count, count - steps))
    return lax.ppermute(value, axis, [(source, source + steps) for source in range(first, last)])


def normalize(states, gains):
    values = states.astype(jnp.float32)
    average = jnp.mean(values, axis=-1, keepdims=True)
    centred = values - average
    spread = jnp.mean(centred * centred, axis=-1, keepdims=True)
    return (centred * lax.rsqrt(spread + epsilon) * gains).astype(jnp.bfloat16)


def project(inputs, weight):
    return jnp.dot(inputs, weight, preferred_element_type=jnp.float32).astype(jnp.bfloat16)


def attend(queries, key_rows, values, key_ok):
    batch_count, row_count, head_width = queries.shape
    key_count = key_rows.shape[1]
    head_count = head_width // HEAD_DIM
    query_heads = queries.reshape(batch_count, row_count, head_count, HEAD_DIM)
    key_heads = key_rows.reshape(batch_count, key_count, head_count, HEAD_DIM)
    value_heads = values.reshape(batch_count, key_count, head_count, HEAD_DIM)
    scores = jnp.einsum(
        "brhd,bkhd->bhrk", query_heads, key_heads, preferred_element_type=jnp.float32
    ) * HEAD_DIM ** (-0.5)
    if key_ok is not None:
        scores = jnp.where(key_ok[:, None, None, :], scores, -1e30)
    highest = jnp.max(scores, axis=-1, keepdims=True)
    weights = jnp.exp(scores - highest)
    chances = (weights / jnp.sum(weights, axis=-1, keepdims=True)).astype(jnp.bfloat16)
    blended = jnp.einsum(
        "bhrk,bkhd->brhd", chances, value_heads, preferred_element_type=jnp.float32
    )
    return blended.astype(jnp.bfloat16).reshape(batch_count * row_count, head_width)


def window(inputs, fetch):
    pieces = []
    for offset in range(-REACH, REACH + 1):
        pieces.append(inputs if offset == 0 else fetch(inputs, offset))
    return jnp.concatenate(pieces, axis=0)


def pick(beside_all, listed, window_start):
    blocks = beside_all.reshape(-1, BLOCK, beside_all.shape[1])
    local_ids = listed - window_start
    chosen = jnp.take(blocks, local_ids, axis=0)
    return chosen.reshape(listed.shape[0], listed.shape[1] * BLOCK, beside_all.shape[1])


def keys_values(normed, key_weight, value_weight):
    return jnp.concatenate([project(normed, key_weight), project(normed, value_weight)], axis=1)


def listed_valid(listed, grid_count):
    every_block = jnp.arange(grid_count.shape[0])
    counts = jnp.sum(
        jnp.where(listed[:, :, None] == every_block[None, None, :], grid_count[None, None, :], 0),
        axis=-1,
    )
    return jnp.arange(BLOCK)[None, None, :] < counts[:, :, None]


def per_device(
    grid_in,
    mesh_in,
    w_query,
    w_key,
    w_value,
    w_out,
    norm_gains,
    enc_list,
    proc_list,
    dec_list,
    grid_count,
):
    node_index = lax.axis_index("nodes")
    head_width = w_query.shape[2]
    grid_blocks = grid_in.shape[0] // BLOCK
    mesh_blocks = mesh_in.shape[0] // BLOCK
    grid_full, mesh_full = (
        lax.all_gather(grid_in, "mp", axis=1, tiled=True),
        lax.all_gather(mesh_in, "mp", axis=1, tiled=True),
    )
    own_counts = lax.dynamic_slice_in_dim(grid_count, node_index * grid_blocks, grid_blocks)
    row_ok = (jnp.arange(BLOCK)[None, :] < own_counts[:, None]).reshape(-1, 1)

    def mesh_update(blended, layer_index, state_part):
        whole_new = None
        terms = jnp.dot(blended, w_out[layer_index], preferred_element_type=jnp.float32)
        shares = summed_on_arrival(terms.astype(jnp.bfloat16), "mp", 1)
        part_new = (state_part.astype(jnp.float32) + shares).astype(jnp.bfloat16)
        whole_new = lax.all_gather(part_new, "mp", axis=1, tiled=True)
        return (part_new, whole_new)

    mesh_queries = project(normalize(mesh_full, norm_gains[0]), w_query[0]).reshape(
        mesh_blocks, BLOCK, head_width
    )
    grid_normed = normalize(grid_full, norm_gains[1])
    grid_kv = keys_values(grid_normed, w_key[0], w_value[0])
    listed_ok = listed_valid(enc_list, grid_count).reshape(enc_list.shape[0], -1)
    beside_all = window(grid_kv, lambda inputs, offset: from_behind(inputs, "nodes", -offset))
    chosen = pick(beside_all, enc_list, (node_index - REACH) * grid_blocks)
    blended = attend(mesh_queries, chosen[:, :, :head_width], chosen[:, :, head_width:], listed_ok)
    state_part, state_whole = mesh_update(blended, 0, mesh_in)
    for layer_index in (1, 2):
        normed = normalize(state_whole, norm_gains[layer_index + 1])
        queries = project(normed, w_query[layer_index]).reshape(mesh_blocks, BLOCK, head_width)
        mesh_kv = keys_values(normed, w_key[layer_index], w_value[layer_index])
        beside_all = window(mesh_kv, lambda inputs, offset: from_behind(inputs, "nodes", -offset))
        chosen = pick(beside_all, proc_list, (node_index - REACH) * mesh_blocks)
        blended = attend(queries, chosen[:, :, :head_width], chosen[:, :, head_width:], None)
        state_part, state_whole = mesh_update(blended, layer_index, state_part)
    grid_queries = project(normalize(grid_full, norm_gains[4]), w_query[3]).reshape(
        grid_blocks, BLOCK, head_width
    )
    mesh_normed = normalize(state_whole, norm_gains[5])
    mesh_kv = keys_values(mesh_normed, w_key[3], w_value[3])
    beside_all = window(mesh_kv, lambda inputs, offset: from_behind(inputs, "nodes", -offset))
    chosen = pick(beside_all, dec_list, (node_index - REACH) * mesh_blocks)
    blended = attend(grid_queries, chosen[:, :, :head_width], chosen[:, :, head_width:], None)
    terms = jnp.dot(blended, w_out[3], preferred_element_type=jnp.float32)
    update = lax.psum_scatter(
        terms.astype(jnp.bfloat16), "mp", scatter_dimension=1, tiled=True
    ).astype(jnp.float32)
    grid_out = grid_in.astype(jnp.float32) + update
    grid_out = jnp.where(row_ok, grid_out, 0.0).astype(jnp.bfloat16)
    return (grid_out, state_part)


def solution(mesh):
    placed = (
        P("nodes", "mp"),
        P("nodes", "mp"),
        P(None, None, "mp"),
        P(None, None, "mp"),
        P(None, None, "mp"),
        P(None, "mp", None),
        P(),
        P("nodes", None),
        P("nodes", None),
        P("nodes", None),
        P(),
    )
    return jax.shard_map(
        per_device,
        mesh=mesh,
        in_specs=placed,
        out_specs=(P("nodes", "mp"), P("nodes", "mp")),
        check_vma=False,
    )
```

profile of v0, /device:TPU:1, one launch (start us, length us, event | category | flops | bytes accessed | tf_op | source)
XLA Modules:
  0.0 329.7 jit_solution(16877713221942611837)
XLA Ops:
  8.8 11.4 %all_gather.16 = bf16[256,1024]{1,0:T(8,128)(2,1)S(1)} all-gather(bf16[256,256]{1,0:T(8,128)(2,1)} %param.14), channel_id=1, replica_groups=mesh['nodes'=128,'mp'=4] {'mp'}, dimensions={1}, use_global_device_ids=true | all-gather | bytes 655360 | tf_op jit(solution)/shard_map/all_gather | solution.py:109
  20.8 1.6 fusion.139
  22.4 1.3 convolution_convert_fusion.18
  23.7 31.9 %all-gather.2.cloned.1.call-done = bf16[1024,1024]{1,0:T(8,128)(2,1)} async-done(((bf16[1024,256]{1,0:T(8,128)(2,1)}), bf16[1024,1024]{1,0:T(8,128)(2,1)}) %all-gather.2.cloned.1.call-update) | async-done | bytes 2097168 | tf_op jit(solution)/shard_map/all_gather | solution.py:108
  55.7 2.1 convert_reduce_fusion
  59.3 1.8 convolution_convert_fusion.5
  61.1 1.8 convolution_convert_fusion.6
  62.9 5.0 %collective-permute-start.1 = (bf16[1024,256]{0,1:T(8,128)(2,1)S(1)}, bf16[1024,256]{0,1:T(8,128)(2,1)}, u32[]{:S(2)}, u32[]{:S(2)}) collective-permute-start(bf16[1024,256]{0,1:T(8,128)(2,1)S(1)} %pad_maximum_fusion), channel_id=1, source_target_pairs={{0,4},{4,8},{8,12},{12,16},{16,20},{20,24},{24,28},{28,32},{32,36}... | collective-permute-start | bytes 1572872 | tf_op jit(solution)/shard_map/ppermute | solution.py:27
  68.0 3.9 %collective-permute-start = (bf16[1024,256]{0,1:T(8,128)(2,1)S(1)}, bf16[1024,256]{0,1:T(8,128)(2,1)}, u32[]{:S(2)}, u32[]{:S(2)}) collective-permute-start(bf16[1024,256]{0,1:T(8,128)(2,1)S(1)} %pad_maximum_fusion), channel_id=1, source_target_pairs={{0,8},{4,12},{8,16},{12,20},{16,24},{20,28},{24,32},{28,36},{32,40... | collective-permute-start | bytes 1572872 | tf_op jit(solution)/shard_map/ppermute | solution.py:27
  71.9 1.9 collective-permute-start.2
  75.4 9.9 %collective-permute-done = bf16[1024,256]{0,1:T(8,128)(2,1)} collective-permute-done((bf16[1024,256]{0,1:T(8,128)(2,1)S(1)}, bf16[1024,256]{0,1:T(8,128)(2,1)}, u32[]{:S(2)}, u32[]{:S(2)}) %collective-permute-start) | collective-permute-done | bytes 524320 | tf_op jit(solution)/shard_map/ppermute | solution.py:27
  85.3 1.9 constant_dynamic-update-slice_fusion.4
  87.2 1.9 constant_dynamic-update-slice_fusion.3
  90.0 1.9 constant_dynamic-update-slice_fusion.1
  91.9 1.9 constant_dynamic-update-slice_fusion
  93.8 4.4 %copy.97 = bf16[5120,256]{1,0:T(8,128)(2,1)} copy(bf16[5120,256]{0,1:T(8,128)(2,1)} %constant_dynamic-update-slice_fusion) | data formatting | bytes 5242880 | tf_op jit(solution)/shard_map/reshape | solution.py:71
  98.2 2.3 gather_fusion
  103.6 2.0 fusion.36
  107.8 3.7 %all-to-all-start = ((bf16[4,256,256]{2,1,0:T(8,128)(2,1)}), bf16[4,256,256]{2,1,0:T(8,128)(2,1)S(1)}, u32[]{:S(2)}, u32[]{:S(2)}) async-start(bf16[4,256,256]{2,1,0:T(8,128)(2,1)} %bitcast.165), calls=%async_computation | async-start | bytes 1048576 | tf_op jit(solution)/shard_map/all_to_all | solution.py:20
  112.9 5.5 %all-to-all-done = bf16[4,256,256]{2,1,0:T(8,128)(2,1)S(1)} async-done(((bf16[4,256,256]{2,1,0:T(8,128)(2,1)}), bf16[4,256,256]{2,1,0:T(8,128)(2,1)S(1)}, u32[]{:S(2)}, u32[]{:S(2)}) %all-to-all-start) | async-done | bytes 524320 | tf_op jit(solution)/shard_map/all_to_all | solution.py:20
  118.5 10.1 %all_gather.17 = bf16[256,1024]{1,0:T(8,128)(2,1)S(1)} all-gather(bf16[256,256]{1,0:T(8,128)(2,1)S(1)} %add_convert_fusion.2), channel_id=1, replica_groups=mesh['nodes'=128,'mp'=4] {'mp'}, dimensions={1}, use_global_device_ids=true | all-gather | bytes 655360 | tf_op jit(solution)/shard_map/all_gather | solution.py:119
  131.9 10.9 %collective-permute-start.5 = (bf16[256,256]{0,1:T(8,128)(2,1)S(1)}, bf16[256,256]{0,1:T(8,128)(2,1)S(1)}, u32[]{:S(2)}, u32[]{:S(2)}) collective-permute-start(bf16[256,256]{0,1:T(8,128)(2,1)S(1)} %pad_maximum_fusion.1), channel_id=1, source_target_pairs={{0,4},{4,8},{8,12},{12,16},{16,20},{20,24},{24,28},{28,32},{32,36}... | collective-permute-start | bytes 393224 | tf_op jit(solution)/shard_map/ppermute | solution.py:27
  142.9 3.2 collective-permute-start.4
  148.6 1.9 collective-permute-start.6
  153.3 2.1 collective-permute-done.6
  156.8 1.4 copy.77
  159.1 1.4 fusion.143
  163.3 10.8 %all_to_all.15 = bf16[4,256,256]{2,1,0:T(8,128)(2,1)S(1)} all-to-all(bf16[4,256,256]{2,1,0:T(8,128)(2,1)S(1)} %bitcast.173), channel_id=1, replica_groups=mesh['nodes'=128,'mp'=4] {'mp'}, dimensions={0} | all-to-all | bytes 1048576 | tf_op jit(solution)/shard_map/all_to_all | solution.py:20
  174.2 11.8 %all_gather.18 = bf16[256,1024]{1,0:T(8,128)(2,1)S(1)} all-gather(bf16[256,256]{1,0:T(8,128)(2,1)S(1)} %add_convert_fusion.1), channel_id=1, replica_groups=mesh['nodes'=128,'mp'=4] {'mp'}, dimensions={1}, use_global_device_ids=true | all-gather | bytes 655360 | tf_op jit(solution)/shard_map/all_gather | solution.py:119
  189.4 5.1 %collective-permute-start.9 = (bf16[256,256]{0,1:T(8,128)(2,1)S(1)}, bf16[256,256]{0,1:T(8,128)(2,1)S(1)}, u32[]{:S(2)}, u32[]{:S(2)}) collective-permute-start(bf16[256,256]{0,1:T(8,128)(2,1)S(1)} %pad_maximum_fusion.2), channel_id=1, source_target_pairs={{0,4},{4,8},{8,12},{12,16},{16,20},{20,24},{24,28},{28,32},{32,36}... | collective-permute-start | bytes 393224 | tf_op jit(solution)/shard_map/ppermute | solution.py:27
  194.5 4.2 %collective-permute-start.8 = (bf16[256,256]{0,1:T(8,128)(2,1)S(1)}, bf16[256,256]{0,1:T(8,128)(2,1)S(1)}, u32[]{:S(2)}, u32[]{:S(2)}) collective-permute-start(bf16[256,256]{0,1:T(8,128)(2,1)S(1)} %pad_maximum_fusion.2), channel_id=1, source_target_pairs={{0,8},{4,12},{8,16},{12,20},{16,24},{20,28},{24,32},{28,36},{32,40... | collective-permute-start | bytes 393224 | tf_op jit(solution)/shard_map/ppermute | solution.py:27
  201.2 1.9 collective-permute-start.10
  205.3 2.3 collective-permute-done.10
  208.9 1.3 copy.84
  215.4 3.5 %all-to-all-start.2 = ((bf16[4,256,256]{2,1,0:T(8,128)(2,1)}), bf16[4,256,256]{2,1,0:T(8,128)(2,1)S(1)}, u32[]{:S(2)}, u32[]{:S(2)}) async-start(bf16[4,256,256]{2,1,0:T(8,128)(2,1)} %bitcast.161), calls=%async_computation.2 | async-start | bytes 1048576 | tf_op jit(solution)/shard_map/all_to_all | solution.py:20
  219.0 7.6 %all-to-all-done.2 = bf16[4,256,256]{2,1,0:T(8,128)(2,1)S(1)} async-done(((bf16[4,256,256]{2,1,0:T(8,128)(2,1)}), bf16[4,256,256]{2,1,0:T(8,128)(2,1)S(1)}, u32[]{:S(2)}, u32[]{:S(2)}) %all-to-all-start.2) | async-done | bytes 524320 | tf_op jit(solution)/shard_map/all_to_all | solution.py:20
  226.7 11.1 %all_gather.19 = bf16[256,1024]{1,0:T(8,128)(2,1)S(1)} all-gather(bf16[256,256]{1,0:T(8,128)(2,1)S(1)} %add_convert_fusion), channel_id=1, replica_groups=mesh['nodes'=128,'mp'=4] {'mp'}, dimensions={1}, use_global_device_ids=true | all-gather | bytes 655360 | tf_op jit(solution)/shard_map/all_gather | solution.py:119
  238.3 1.4 convolution_convert_fusion.7
  239.6 1.4 convolution_convert_fusion.8
  241.0 4.5 %collective-permute-start.13 = (bf16[256,256]{0,1:T(8,128)(2,1)S(1)}, bf16[256,256]{0,1:T(8,128)(2,1)S(1)}, u32[]{:S(2)}, u32[]{:S(2)}) collective-permute-start(bf16[256,256]{0,1:T(8,128)(2,1)S(1)} %pad_maximum_fusion.3), channel_id=1, source_target_pairs={{0,4},{4,8},{8,12},{12,16},{16,20},{20,24},{24,28},{28,32},{32,36}... | collective-permute-start | bytes 393224 | tf_op jit(solution)/shard_map/ppermute | solution.py:27
  245.5 5.6 %collective-permute-start.12 = (bf16[256,256]{0,1:T(8,128)(2,1)S(1)}, bf16[256,256]{0,1:T(8,128)(2,1)S(1)}, u32[]{:S(2)}, u32[]{:S(2)}) collective-permute-start(bf16[256,256]{0,1:T(8,128)(2,1)S(1)} %pad_maximum_fusion.3), channel_id=1, source_target_pairs={{0,8},{4,12},{8,16},{12,20},{16,24},{20,28},{24,32},{28,36},{32,40... | collective-permute-start | bytes 393224 | tf_op jit(solution)/shard_map/ppermute | solution.py:27
  251.2 1.8 fusion.32
  255.3 1.9 collective-permute-start.14
  257.3 5.2 %collective-permute-done.14 = bf16[256,256]{0,1:T(8,128)(2,1)S(1)} collective-permute-done((bf16[256,256]{0,1:T(8,128)(2,1)S(1)}, bf16[256,256]{0,1:T(8,128)(2,1)S(1)}, u32[]{:S(2)}, u32[]{:S(2)}) %collective-permute-start.14) | collective-permute-done | bytes 131104 | tf_op jit(solution)/shard_map/ppermute | solution.py:27
  266.4 3.7 %fusion.35 = bf16[8,128,2,64]{1,3,2,0:T(8,128)(2,1)S(1)} fusion(bf16[8,256,2,64]{1,3,2,0:T(8,128)(2,1)S(1)} %bitcast.190, f32[8,2,128]{2,1,0:T(2,128)S(1)} %fusion.149, bf16[8,256,2,64]{1,3,2,0:T(8,128)(2,1)S(1)} %bitcast.189, bf16[8,128,2,64]{3,2,1,0:T(2,128)(2,1)S(1)} %copy-done.3), kind=kOutput, calls=%fused_computation.59 | convolution fusion | flops 136448256 | bytes 1581056 | tf_op jit(solution)/shard_map/bhrk,bkhd->brhd/dot_general | solution.py:57
  270.3 3.0 convolution_convert_fusion
  274.2 46.6 %reduce-scatter.2.cloned.1.call-done = bf16[1024,256]{1,0:T(8,128)(2,1)} async-done(((bf16[1024,1024]{1,0:T(8,128)(2,1)}), bf16[1024,256]{1,0:T(8,128)(2,1)}) %reduce-scatter.2.cloned.1.call-update) | async-done | bytes 524304 | tf_op jit(solution)/shard_map/reduce_scatter | solution.py:149
  320.9 2.0 select_convert_fusion
  (166 shorter events, 49.0 us)
Async XLA Ops:
  7.2 48.5 %all-gather.2.cloned.1.call-start = ((), (), s32[]{:S(2)}) async-start(), calls=%async_computation.4 | async-start | bytes 2621440 | tf_op jit(solution)/shard_map/all_gather | solution.py:108
  20.8 80.7 %copy-start.8 = (pred[2,512]{1,0:T(4,128)(4,1)}, pred[2,512]{1,0:T(4,128)(4,1)S(1)}, u32[]{:S(2)}) copy-start(pred[2,512]{1,0:T(4,128)(4,1)S(1)} %bitcast_compare_fusion) | copy-start | bytes 3076
  55.7 2.2 copy-start
  59.3 12.6 %copy-start.13 = (s32[2,4]{1,0:T(2,128)S(1)}, s32[2,4]{1,0:T(2,128)}, u32[]{:S(2)}) copy-start(s32[2,4]{1,0:T(2,128)} %param.20) | copy-start | bytes 100
  62.9 24.3 %collective-permute-start.1 = (bf16[1024,256]{0,1:T(8,128)(2,1)S(1)}, bf16[1024,256]{0,1:T(8,128)(2,1)}, u32[]{:S(2)}, u32[]{:S(2)}) collective-permute-start(bf16[1024,256]{0,1:T(8,128)(2,1)S(1)} %pad_maximum_fusion), channel_id=1, source_target_pairs={{0,4},{4,8},{8,12},{12,16},{16,20},{20,24},{24,28},{28,32},{32,36}... | collective-permute-start | bytes 1572872 | tf_op jit(solution)/shard_map/ppermute | solution.py:27
  68.0 17.3 %collective-permute-start = (bf16[1024,256]{0,1:T(8,128)(2,1)S(1)}, bf16[1024,256]{0,1:T(8,128)(2,1)}, u32[]{:S(2)}, u32[]{:S(2)}) collective-permute-start(bf16[1024,256]{0,1:T(8,128)(2,1)S(1)} %pad_maximum_fusion), channel_id=1, source_target_pairs={{0,8},{4,12},{8,16},{12,20},{16,24},{20,28},{24,32},{28,36},{32,40... | collective-permute-start | bytes 1572872 | tf_op jit(solution)/shard_map/ppermute | solution.py:27
  71.9 18.1 %collective-permute-start.2 = (bf16[1024,256]{0,1:T(8,128)(2,1)S(1)}, bf16[1024,256]{0,1:T(8,128)(2,1)}, u32[]{:S(2)}, u32[]{:S(2)}) collective-permute-start(bf16[1024,256]{0,1:T(8,128)(2,1)S(1)} %pad_maximum_fusion), channel_id=1, source_target_pairs={{4,0},{8,4},{12,8},{16,12},{20,16},{24,20},{28,24},{32,28},{36,32}... | collective-permute-start | bytes 1572872 | tf_op jit(solution)/shard_map/ppermute | solution.py:27
  73.9 17.9 %collective-permute-start.3 = (bf16[1024,256]{0,1:T(8,128)(2,1)S(1)}, bf16[1024,256]{0,1:T(8,128)(2,1)}, u32[]{:S(2)}, u32[]{:S(2)}) collective-permute-start(bf16[1024,256]{0,1:T(8,128)(2,1)S(1)} %pad_maximum_fusion), channel_id=1, source_target_pairs={{8,0},{12,4},{16,8},{20,12},{24,16},{28,20},{32,24},{36,28},{40,32... | collective-permute-start | bytes 1572872 | tf_op jit(solution)/shard_map/ppermute | solution.py:27
  105.6 5.9 %copy-start.15 = (s32[2,3]{1,0:T(2,128)S(1)}, s32[2,3]{1,0:T(2,128)}, u32[]{:S(2)}) copy-start(s32[2,3]{1,0:T(2,128)} %param.21) | copy-start | bytes 76
  105.6 6.0 %copy-start.16 = (s32[8,2]{0,1:T(2,128)S(1)}, s32[8,2]{0,1:T(2,128)}, u32[]{:S(2)}) copy-start(s32[8,2]{0,1:T(2,128)} %param.22) | copy-start | bytes 196
  105.6 12.9 %copy-start.4 = (bf16[256,256]{1,0:T(8,128)(2,1)S(1)}, bf16[256,256]{1,0:T(8,128)(2,1)}, u32[]{:S(2)}) copy-start(bf16[256,256]{1,0:T(8,128)(2,1)} %param.14) | copy-start | bytes 393220
  107.8 10.6 %all-to-all-start = ((bf16[4,256,256]{2,1,0:T(8,128)(2,1)}), bf16[4,256,256]{2,1,0:T(8,128)(2,1)S(1)}, u32[]{:S(2)}, u32[]{:S(2)}) async-start(bf16[4,256,256]{2,1,0:T(8,128)(2,1)} %bitcast.165), calls=%async_computation | async-start | bytes 1048576 | tf_op jit(solution)/shard_map/all_to_all | solution.py:20
  111.5 47.2 %copy-start.9 = (pred[2,3]{1,0:T(4,128)(4,1)}, pred[2,3]{1,0:T(4,128)(4,1)S(1)}, u32[]{:S(2)}) copy-start(pred[2,3]{1,0:T(4,128)(4,1)S(1)} %get-tuple-element.5) | copy-start | bytes 22
  112.9 45.3 %copy-start.7 = (s32[1024]{0:T(1024)}, s32[1024]{0:T(1024)S(1)}, u32[]{:S(2)}) copy-start(s32[1024]{0:T(1024)S(1)} %get-tuple-element.24) | copy-start | bytes 12292
  131.9 20.0 %collective-permute-start.5 = (bf16[256,256]{0,1:T(8,128)(2,1)S(1)}, bf16[256,256]{0,1:T(8,128)(2,1)S(1)}, u32[]{:S(2)}, u32[]{:S(2)}) collective-permute-start(bf16[256,256]{0,1:T(8,128)(2,1)S(1)} %pad_maximum_fusion.1), channel_id=1, source_target_pairs={{0,4},{4,8},{8,12},{12,16},{16,20},{20,24},{24,28},{28,32},{32,36}... | collective-permute-start | bytes 393224 | tf_op jit(solution)/shard_map/ppermute | solution.py:27
  142.9 8.4 %collective-permute-start.4 = (bf16[256,256]{0,1:T(8,128)(2,1)S(1)}, bf16[256,256]{0,1:T(8,128)(2,1)S(1)}, u32[]{:S(2)}, u32[]{:S(2)}) collective-permute-start(bf16[256,256]{0,1:T(8,128)(2,1)S(1)} %pad_maximum_fusion.1), channel_id=1, source_target_pairs={{0,8},{4,12},{8,16},{12,20},{16,24},{20,28},{24,32},{28,36},{32,40... | collective-permute-start | bytes 393224 | tf_op jit(solution)/shard_map/ppermute | solution.py:27
  147.3 8.8 %collective-permute-start.7 = (bf16[256,256]{0,1:T(8,128)(2,1)S(1)}, bf16[256,256]{0,1:T(8,128)(2,1)S(1)}, u32[]{:S(2)}, u32[]{:S(2)}) collective-permute-start(bf16[256,256]{0,1:T(8,128)(2,1)S(1)} %pad_maximum_fusion.1), channel_id=1, source_target_pairs={{8,0},{12,4},{16,8},{20,12},{24,16},{28,20},{32,24},{36,28},{40,32... | collective-permute-start | bytes 393224 | tf_op jit(solution)/shard_map/ppermute | solution.py:27
  148.6 6.8 %collective-permute-start.6 = (bf16[256,256]{0,1:T(8,128)(2,1)S(1)}, bf16[256,256]{0,1:T(8,128)(2,1)S(1)}, u32[]{:S(2)}, u32[]{:S(2)}) collective-permute-start(bf16[256,256]{0,1:T(8,128)(2,1)S(1)} %pad_maximum_fusion.1), channel_id=1, source_target_pairs={{4,0},{8,4},{12,8},{16,12},{20,16},{24,20},{28,24},{32,28},{36,32}... | collective-permute-start | bytes 393224 | tf_op jit(solution)/shard_map/ppermute | solution.py:27
  156.8 3.7 %copy-start.2 = (bf16[2,128,2,64]{3,2,1,0:T(2,128)(2,1)S(1)}, bf16[2,128,2,64]{3,2,1,0:T(2,128)(2,1)}, u32[]{:S(2)}) copy-start(bf16[2,128,2,64]{3,2,1,0:T(2,128)(2,1)} %reshape.261) | copy-start | bytes 196612
  188.1 22.8 %copy-start.10 = (pred[2,3]{1,0:T(4,128)(4,1)S(1)}, pred[2,3]{1,0:T(4,128)(4,1)}, u32[]{:S(2)}) copy-start(pred[2,3]{1,0:T(4,128)(4,1)} %copy-done.9) | copy-start | bytes 22
  189.4 14.5 %collective-permute-start.9 = (bf16[256,256]{0,1:T(8,128)(2,1)S(1)}, bf16[256,256]{0,1:T(8,128)(2,1)S(1)}, u32[]{:S(2)}, u32[]{:S(2)}) collective-permute-start(bf16[256,256]{0,1:T(8,128)(2,1)S(1)} %pad_maximum_fusion.2), channel_id=1, source_target_pairs={{0,4},{4,8},{8,12},{12,16},{16,20},{20,24},{24,28},{28,32},{32,36}... | collective-permute-start | bytes 393224 | tf_op jit(solution)/shard_map/ppermute | solution.py:27
  194.5 8.8 %collective-permute-start.8 = (bf16[256,256]{0,1:T(8,128)(2,1)S(1)}, bf16[256,256]{0,1:T(8,128)(2,1)S(1)}, u32[]{:S(2)}, u32[]{:S(2)}) collective-permute-start(bf16[256,256]{0,1:T(8,128)(2,1)S(1)} %pad_maximum_fusion.2), channel_id=1, source_target_pairs={{0,8},{4,12},{8,16},{12,20},{16,24},{20,28},{24,32},{28,36},{32,40... | collective-permute-start | bytes 393224 | tf_op jit(solution)/shard_map/ppermute | solution.py:27
  199.9 8.3 %collective-permute-start.11 = (bf16[256,256]{0,1:T(8,128)(2,1)S(1)}, bf16[256,256]{0,1:T(8,128)(2,1)S(1)}, u32[]{:S(2)}, u32[]{:S(2)}) collective-permute-start(bf16[256,256]{0,1:T(8,128)(2,1)S(1)} %pad_maximum_fusion.2), channel_id=1, source_target_pairs={{8,0},{12,4},{16,8},{20,12},{24,16},{28,20},{32,24},{36,28},{40,32... | collective-permute-start | bytes 393224 | tf_op jit(solution)/shard_map/ppermute | solution.py:27
  201.2 6.4 %collective-permute-start.10 = (bf16[256,256]{0,1:T(8,128)(2,1)S(1)}, bf16[256,256]{0,1:T(8,128)(2,1)S(1)}, u32[]{:S(2)}, u32[]{:S(2)}) collective-permute-start(bf16[256,256]{0,1:T(8,128)(2,1)S(1)} %pad_maximum_fusion.2), channel_id=1, source_target_pairs={{4,0},{8,4},{12,8},{16,12},{20,16},{24,20},{28,24},{32,28},{36,32}... | collective-permute-start | bytes 393224 | tf_op jit(solution)/shard_map/ppermute | solution.py:27
  212.2 6.8 %copy-start.14 = (pred[8,2]{0,1:T(4,128)(4,1)S(1)}, pred[8,2]{0,1:T(4,128)(4,1)}, u32[]{:S(2)}) copy-start(pred[8,2]{0,1:T(4,128)(4,1)} %get-tuple-element.3) | copy-start | bytes 52
  214.6 23.7 %copy-start.12 = (f32[1,1024]{1,0:T(1,128)S(1)}, f32[1,1024]{1,0:T(1,128)}, u32[]{:S(2)}) copy-start(f32[1,1024]{1,0:T(1,128)} %get-tuple-element.22) | copy-start | bytes 12292
  215.4 11.2 %all-to-all-start.2 = ((bf16[4,256,256]{2,1,0:T(8,128)(2,1)}), bf16[4,256,256]{2,1,0:T(8,128)(2,1)S(1)}, u32[]{:S(2)}, u32[]{:S(2)}) async-start(bf16[4,256,256]{2,1,0:T(8,128)(2,1)} %bitcast.161), calls=%async_computation.2 | async-start | bytes 1048576 | tf_op jit(solution)/shard_map/all_to_all | solution.py:20
  218.9 102.0 %reduce-scatter.2.cloned.1.call-start = ((), (), s32[]{:S(2)}) async-start(), calls=%async_computation.5 | async-start | bytes 2621440 | tf_op jit(solution)/shard_map/reduce_scatter | solution.py:149
  226.7 26.3 %copy-start.5 = (bf16[256,256]{1,0:T(8,128)(2,1)}, bf16[256,256]{1,0:T(8,128)(2,1)S(1)}, u32[]{:S(2)}) copy-start(bf16[256,256]{1,0:T(8,128)(2,1)S(1)} %add_convert_fusion) | copy-start | bytes 393220
  226.7 24.4 %copy-start.11 = (f32[1,1024]{1,0:T(1,128)S(1)}, f32[1,1024]{1,0:T(1,128)}, u32[]{:S(2)}) copy-start(f32[1,1024]{1,0:T(1,128)} %get-tuple-element.17) | copy-start | bytes 12292
  241.0 16.2 %collective-permute-start.13 = (bf16[256,256]{0,1:T(8,128)(2,1)S(1)}, bf16[256,256]{0,1:T(8,128)(2,1)S(1)}, u32[]{:S(2)}, u32[]{:S(2)}) collective-permute-start(bf16[256,256]{0,1:T(8,128)(2,1)S(1)} %pad_maximum_fusion.3), channel_id=1, source_target_pairs={{0,4},{4,8},{8,12},{12,16},{16,20},{20,24},{24,28},{28,32},{32,36}... | collective-permute-start | bytes 393224 | tf_op jit(solution)/shard_map/ppermute | solution.py:27
  245.5 11.7 %collective-permute-start.12 = (bf16[256,256]{0,1:T(8,128)(2,1)S(1)}, bf16[256,256]{0,1:T(8,128)(2,1)S(1)}, u32[]{:S(2)}, u32[]{:S(2)}) collective-permute-start(bf16[256,256]{0,1:T(8,128)(2,1)S(1)} %pad_maximum_fusion.3), channel_id=1, source_target_pairs={{0,8},{4,12},{8,16},{12,20},{16,24},{20,28},{24,32},{28,36},{32,40... | collective-permute-start | bytes 393224 | tf_op jit(solution)/shard_map/ppermute | solution.py:27
  253.0 10.3 %copy-start.6 = (s32[1024]{0:T(1024)S(1)}, s32[1024]{0:T(1024)}, u32[]{:S(2)}) copy-start(s32[1024]{0:T(1024)} %get-tuple-element.23) | copy-start | bytes 12292
  254.0 9.0 %collective-permute-start.15 = (bf16[256,256]{0,1:T(8,128)(2,1)S(1)}, bf16[256,256]{0,1:T(8,128)(2,1)S(1)}, u32[]{:S(2)}, u32[]{:S(2)}) collective-permute-start(bf16[256,256]{0,1:T(8,128)(2,1)S(1)} %pad_maximum_fusion.3), channel_id=1, source_target_pairs={{8,0},{12,4},{16,8},{20,12},{24,16},{28,20},{32,24},{36,28},{40,32... | collective-permute-start | bytes 393224 | tf_op jit(solution)/shard_map/ppermute | solution.py:27
  255.3 7.2 %collective-permute-start.14 = (bf16[256,256]{0,1:T(8,128)(2,1)S(1)}, bf16[256,256]{0,1:T(8,128)(2,1)S(1)}, u32[]{:S(2)}, u32[]{:S(2)}) collective-permute-start(bf16[256,256]{0,1:T(8,128)(2,1)S(1)} %pad_maximum_fusion.3), channel_id=1, source_target_pairs={{4,0},{8,4},{12,8},{16,12},{20,16},{24,20},{28,24},{32,28},{36,32}... | collective-permute-start | bytes 393224 | tf_op jit(solution)/shard_map/ppermute | solution.py:27
  264.4 1.0 copy-start.3
  270.1 50.7 %copy-start.1 = (bf16[1024,256]{1,0:T(8,128)(2,1)S(1)}, bf16[1024,256]{1,0:T(8,128)(2,1)}, u32[]{:S(2)}) copy-start(bf16[1024,256]{1,0:T(8,128)(2,1)} %param.13) | copy-start | bytes 1572868
Sparse Core Ops, SparseCore 0:
  10.1 45.5 all-gather.1
  273.5 47.2 reduce-scatter.1
where the time goes:
time: 332 us; the launch traced here: 330 us
  waiting for transfers between devices  112 us (34%)
  starting transfers between devices  62.4 us (19%)
  blocking collectives  55.2 us (17%)
  matrix products  36.8 us (11%)
  local copies, waits for them, and re-layouts  35 us (11%)
  between operations  14.9 us (4%)
  other arithmetic  13.1 us (4%)
    ppermute x16, starting transfers between devices, from_behind(): lax.ppermute(value, axis, [(source, source + steps) for source in range(f...  55.2 us
    reduce_scatter x1, waiting for transfers between devices, per_device(): lax.psum_scatter(terms.astype(jnp.bfloat16), 'mp', scatter_dimension=1, t...  46.6 us
    all_gather x3, blocking collectives, mesh_update(): whole_new = lax.all_gather(part_new, 'mp', axis=1, tiled=True)  33 us
    all_gather x1, waiting for transfers between devices, per_device(): lax.all_gather(grid_in, 'mp', axis=1, tiled=True)  31.9 us
    ppermute x16, waiting for transfers between devices, from_behind(): lax.ppermute(value, axis, [(source, source + steps) for source in range(f...  20 us
    dot_general x12, matrix products, project(): jnp.dot(inputs, weight, preferred_element_type=jnp.float32)  16.9 us
    all_to_all x2, waiting for transfers between devices, summed_on_arrival(): lax.all_to_all(pieces, axis, split_axis=0, concat_axis=0, tiled=True)  13.1 us
    all_gather x1, blocking collectives, per_device(): lax.all_gather(mesh_in, 'mp', axis=1, tiled=True)  11.4 us
  transfers between devices with their start and end apart: 20, of which 9 were waited for; matrix products, arithmetic and copies ran while one was open for 8% of the time, Pallas kernels for 0%

commit v1 on v0

--- a/solution.py
+++ b/solution.py
@@ -104,8 +104,17 @@
     head_width = w_query.shape[2]
     grid_blocks = grid_in.shape[0] // BLOCK
     mesh_blocks = mesh_in.shape[0] // BLOCK
+    panels_launch = lambda original: jnp.concatenate(
+        jax.lax.all_to_all(
+            jnp.stack(jax.lax.axis_size("mp") * [original], axis=0),
+            axis_name="mp",
+            split_axis=0,
+            concat_axis=0,
+        ),
+        axis=1,
+    )
     grid_full, mesh_full = (
-        lax.all_gather(grid_in, "mp", axis=1, tiled=True),
+        panels_launch(grid_in),
         lax.all_gather(mesh_in, "mp", axis=1, tiled=True),
     )
     own_counts = lax.dynamic_slice_in_dim(grid_count, node_index * grid_blocks, grid_blocks)

time: 332 us -> 310 us (0.934)
  waiting for transfers between devices: 112 us -> 89.5 us
  blocking collectives: 55.2 us -> 71.9 us
  local copies, waits for them, and re-layouts: 35 us -> 19.7 us
  starting transfers between devices: 62.4 us -> 72.3 us
  matrix products: 36.8 us -> 30.3 us
  other arithmetic: 13.1 us -> 9.53 us
    all_gather x1 -> x0, waiting for transfers between devices: 31.9 us -> none  [per_device(): lax.all_gather(grid_in, 'mp', axis=1, tiled=True)]
    all_gather x1, blocking collectives: 11.4 us -> 29.5 us  [per_device(): lax.all_gather(mesh_in, 'mp', axis=1, tiled=True)]
    ppermute x16, waiting for transfers between devices: 20 us -> 26.9 us  [from_behind(): lax.ppermute(value, axis, [(source, source + steps) for source in range(f...]
    unnamed x49 -> x36, local copies, waits for them, and re-layouts: 10.9 us -> 4.8 us
    all_to_all x0 -> x1, starting transfers between devices: none -> 5.14 us  [per_device(): jax.lax.all_to_all(jnp.stack(jax.lax.axis_size('mp') * [original], axis=0...]
    ppermute x16, starting transfers between devices: 55.2 us -> 60.1 us  [from_behind(): lax.ppermute(value, axis, [(source, source + steps) for source in range(f...]
    concatenate x7, local copies, waits for them, and re-layouts: 6.18 us -> 1.82 us  [window(): return jnp.concatenate(pieces, axis=0)]
  transfers between devices with their start and end apart: 20 -> 20, of which waited for: 9 -> 10; matrix products, arithmetic and copies ran while one was open for 8% -> 4% of each run, Pallas kernels for 0% -> 0%
where the time goes in v1:
time: 310 us; the launch traced here: 308 us
  waiting for transfers between devices  89.5 us (29%)
  starting transfers between devices  72.3 us (23%)
  blocking collectives  71.9 us (23%)
  matrix products  30.3 us (10%)
  local copies, waits for them, and re-layouts  19.7 us (6%)
  between operations  14.9 us (5%)
  other arithmetic  9.53 us (3%)
    ppermute x16, starting transfers between devices, from_behind(): lax.ppermute(value, axis, [(source, source + steps) for source in range(f...  60.1 us
    reduce_scatter x1, waiting for transfers between devices, per_device(): lax.psum_scatter(terms.astype(jnp.bfloat16), 'mp', scatter_dimension=1, t...  47.5 us
    all_gather x3, blocking collectives, mesh_update(): whole_new = lax.all_gather(part_new, 'mp', axis=1, tiled=True)  33.1 us
    all_gather x1, blocking collectives, per_device(): lax.all_gather(mesh_in, 'mp', axis=1, tiled=True)  29.5 us
    ppermute x16, waiting for transfers between devices, from_behind(): lax.ppermute(value, axis, [(source, source + steps) for source in range(f...  26.9 us
    dot_general x12, matrix products, project(): jnp.dot(inputs, weight, preferred_element_type=jnp.float32)  16.3 us
    all_to_all x2, waiting for transfers between devices, summed_on_arrival(): lax.all_to_all(pieces, axis, split_axis=0, concat_axis=0, tiled=True)  15 us
    all_to_all x1, blocking collectives, summed_on_arrival(): lax.all_to_all(pieces, axis, split_axis=0, concat_axis=0, tiled=True)  9.33 us
  transfers between devices with their start and end apart: 20, of which 10 were waited for; matrix products, arithmetic and copies ran while one was open for 4% of the time, Pallas kernels for 0%

profile of v1, /device:TPU:1, one launch (start us, length us, event | category | flops | bytes accessed | tf_op | source)
XLA Modules:
  0.0 308.1 jit_solution(10817980402256897691)
XLA Ops:
  8.4 1.6 stack.2
  10.0 5.1 %all-to-all-start = ((bf16[4,1024,256]{1,2,0:T(8,128)(2,1)}), bf16[4,1024,256]{1,2,0:T(8,128)(2,1)S(1)}, u32[]{:S(2)}, u32[]{:S(2)}) async-start(bf16[4,1024,256]{1,2,0:T(8,128)(2,1)} %stack.2), calls=%async_computation | async-start | bytes 4194304 | tf_op jit(solution)/shard_map/all_to_all | solution.py:108
  15.2 29.5 %all_gather.12 = bf16[256,1024]{1,0:T(8,128)(2,1)S(1)} all-gather(bf16[256,256]{1,0:T(8,128)(2,1)S(1)} %copy-done.3), channel_id=1, replica_groups=mesh['nodes'=128,'mp'=4] {'mp'}, dimensions={1}, use_global_device_ids=true | all-gather | bytes 655360 | tf_op jit(solution)/shard_map/all_gather | solution.py:118
  45.5 1.3 convolution_convert_fusion.19
  47.8 2.2 fusion.9
  50.0 1.4 convolution_convert_fusion.6
  51.4 1.4 convolution_convert_fusion.7
  53.7 9.1 %collective-permute-start.1 = (bf16[1024,256]{0,1:T(8,128)(2,1)}, bf16[1024,256]{0,1:T(8,128)(2,1)}, u32[]{:S(2)}, u32[]{:S(2)}) collective-permute-start(bf16[1024,256]{0,1:T(8,128)(2,1)} %pad_maximum_fusion), channel_id=1, source_target_pairs={{0,4},{4,8},{8,12},{12,16},{16,20},{20,24},{24,28},{28,32},{32,36}... | collective-permute-start | bytes 1572872 | tf_op jit(solution)/shard_map/ppermute | solution.py:27
  62.8 3.9 %collective-permute-start = (bf16[1024,256]{0,1:T(8,128)(2,1)}, bf16[1024,256]{0,1:T(8,128)(2,1)}, u32[]{:S(2)}, u32[]{:S(2)}) collective-permute-start(bf16[1024,256]{0,1:T(8,128)(2,1)} %pad_maximum_fusion), channel_id=1, source_target_pairs={{0,8},{4,12},{8,16},{12,20},{16,24},{20,28},{24,32},{28,36},{32,40... | collective-permute-start | bytes 1572872 | tf_op jit(solution)/shard_map/ppermute | solution.py:27
  66.7 1.9 collective-permute-start.2
  68.8 1.3 collective-permute-start.3
  70.2 10.2 %collective-permute-done = bf16[1024,256]{0,1:T(8,128)(2,1)} collective-permute-done((bf16[1024,256]{0,1:T(8,128)(2,1)}, bf16[1024,256]{0,1:T(8,128)(2,1)}, u32[]{:S(2)}, u32[]{:S(2)}) %collective-permute-start) | collective-permute-done | bytes 524320 | tf_op jit(solution)/shard_map/ppermute | solution.py:27
  86.0 2.6 copy.100
  88.6 2.3 gather_fusion
  94.4 3.5 %all-to-all-start.1 = ((bf16[4,256,256]{2,1,0:T(8,128)(2,1)}), bf16[4,256,256]{2,1,0:T(8,128)(2,1)S(1)}, u32[]{:S(2)}, u32[]{:S(2)}) async-start(bf16[4,256,256]{2,1,0:T(8,128)(2,1)} %bitcast.170), calls=%async_computation.1 | async-start | bytes 1048576 | tf_op jit(solution)/shard_map/all_to_all | solution.py:20
  98.2 6.6 %all-to-all-done.1 = bf16[4,256,256]{2,1,0:T(8,128)(2,1)S(1)} async-done(((bf16[4,256,256]{2,1,0:T(8,128)(2,1)}), bf16[4,256,256]{2,1,0:T(8,128)(2,1)S(1)}, u32[]{:S(2)}, u32[]{:S(2)}) %all-to-all-start.1) | async-done | bytes 524320 | tf_op jit(solution)/shard_map/all_to_all | solution.py:20
  104.9 11.0 %all_gather.13 = bf16[256,1024]{1,0:T(8,128)(2,1)S(1)} all-gather(bf16[256,256]{1,0:T(8,128)(2,1)S(1)} %add_convert_fusion.2), channel_id=1, replica_groups=mesh['nodes'=128,'mp'=4] {'mp'}, dimensions={1}, use_global_device_ids=true | all-gather | bytes 655360 | tf_op jit(solution)/shard_map/all_gather | solution.py:128
  116.6 1.3 convolution_convert_fusion.16
  117.9 1.3 convolution_convert_fusion.17
  119.2 9.9 %collective-permute-start.5 = (bf16[256,256]{0,1:T(8,128)(2,1)S(1)}, bf16[256,256]{0,1:T(8,128)(2,1)S(1)}, u32[]{:S(2)}, u32[]{:S(2)}) collective-permute-start(bf16[256,256]{0,1:T(8,128)(2,1)S(1)} %pad_maximum_fusion.1), channel_id=1, source_target_pairs={{0,4},{4,8},{8,12},{12,16},{16,20},{20,24},{24,28},{28,32},{32,36}... | collective-permute-start | bytes 393224 | tf_op jit(solution)/shard_map/ppermute | solution.py:27
  129.1 3.6 %collective-permute-start.4 = (bf16[256,256]{0,1:T(8,128)(2,1)S(1)}, bf16[256,256]{0,1:T(8,128)(2,1)S(1)}, u32[]{:S(2)}, u32[]{:S(2)}) collective-permute-start(bf16[256,256]{0,1:T(8,128)(2,1)S(1)} %pad_maximum_fusion.1), channel_id=1, source_target_pairs={{0,8},{4,12},{8,16},{12,20},{16,24},{20,28},{24,32},{28,36},{32,40... | collective-permute-start | bytes 393224 | tf_op jit(solution)/shard_map/ppermute | solution.py:27
  134.0 1.3 collective-permute-start.7
  135.3 1.9 collective-permute-start.6
  137.4 5.5 %collective-permute-done.6 = bf16[256,256]{0,1:T(8,128)(2,1)S(1)} collective-permute-done((bf16[256,256]{0,1:T(8,128)(2,1)S(1)}, bf16[256,256]{0,1:T(8,128)(2,1)S(1)}, u32[]{:S(2)}, u32[]{:S(2)}) %collective-permute-start.6) | collective-permute-done | bytes 131104 | tf_op jit(solution)/shard_map/ppermute | solution.py:27
  146.6 9.3 %all_to_all.20 = bf16[4,256,256]{2,1,0:T(8,128)(2,1)S(1)} all-to-all(bf16[4,256,256]{2,1,0:T(8,128)(2,1)S(1)} %bitcast.181), channel_id=1, replica_groups=mesh['nodes'=128,'mp'=4] {'mp'}, dimensions={0} | all-to-all | bytes 1048576 | tf_op jit(solution)/shard_map/all_to_all | solution.py:20
  156.0 11.0 %all_gather.14 = bf16[256,1024]{1,0:T(8,128)(2,1)S(1)} all-gather(bf16[256,256]{1,0:T(8,128)(2,1)S(1)} %add_convert_fusion.1), channel_id=1, replica_groups=mesh['nodes'=128,'mp'=4] {'mp'}, dimensions={1}, use_global_device_ids=true | all-gather | bytes 655360 | tf_op jit(solution)/shard_map/all_gather | solution.py:128
  167.8 1.3 convolution_convert_fusion.12
  169.1 1.3 convolution_convert_fusion.13
  170.4 7.4 %collective-permute-start.9 = (bf16[256,256]{0,1:T(8,128)(2,1)S(1)}, bf16[256,256]{0,1:T(8,128)(2,1)S(1)}, u32[]{:S(2)}, u32[]{:S(2)}) collective-permute-start(bf16[256,256]{0,1:T(8,128)(2,1)S(1)} %pad_maximum_fusion.2), channel_id=1, source_target_pairs={{0,4},{4,8},{8,12},{12,16},{16,20},{20,24},{24,28},{28,32},{32,36}... | collective-permute-start | bytes 393224 | tf_op jit(solution)/shard_map/ppermute | solution.py:27
  177.8 4.7 %collective-permute-start.8 = (bf16[256,256]{0,1:T(8,128)(2,1)S(1)}, bf16[256,256]{0,1:T(8,128)(2,1)S(1)}, u32[]{:S(2)}, u32[]{:S(2)}) collective-permute-start(bf16[256,256]{0,1:T(8,128)(2,1)S(1)} %pad_maximum_fusion.2), channel_id=1, source_target_pairs={{0,8},{4,12},{8,16},{12,20},{16,24},{20,28},{24,32},{28,36},{32,40... | collective-permute-start | bytes 393224 | tf_op jit(solution)/shard_map/ppermute | solution.py:27
  183.7 1.3 collective-permute-start.11
  185.0 1.9 collective-permute-start.10
  187.2 4.2 %collective-permute-done.10 = bf16[256,256]{0,1:T(8,128)(2,1)S(1)} collective-permute-done((bf16[256,256]{0,1:T(8,128)(2,1)S(1)}, bf16[256,256]{0,1:T(8,128)(2,1)S(1)}, u32[]{:S(2)}, u32[]{:S(2)}) %collective-permute-start.10) | collective-permute-done | bytes 131104 | tf_op jit(solution)/shard_map/ppermute | solution.py:27
  195.8 3.5 %all-to-all-start.3 = ((bf16[4,256,256]{2,1,0:T(8,128)(2,1)}), bf16[4,256,256]{2,1,0:T(8,128)(2,1)S(1)}, u32[]{:S(2)}, u32[]{:S(2)}) async-start(bf16[4,256,256]{2,1,0:T(8,128)(2,1)} %bitcast.166), calls=%async_computation.3 | async-start | bytes 1048576 | tf_op jit(solution)/shard_map/all_to_all | solution.py:20
  199.4 8.4 %all-to-all-done.3 = bf16[4,256,256]{2,1,0:T(8,128)(2,1)S(1)} async-done(((bf16[4,256,256]{2,1,0:T(8,128)(2,1)}), bf16[4,256,256]{2,1,0:T(8,128)(2,1)S(1)}, u32[]{:S(2)}, u32[]{:S(2)}) %all-to-all-start.3) | async-done | bytes 524320 | tf_op jit(solution)/shard_map/all_to_all | solution.py:20
  207.9 11.1 %all_gather.15 = bf16[256,1024]{1,0:T(8,128)(2,1)S(1)} all-gather(bf16[256,256]{1,0:T(8,128)(2,1)S(1)} %add_convert_fusion), channel_id=1, replica_groups=mesh['nodes'=128,'mp'=4] {'mp'}, dimensions={1}, use_global_device_ids=true | all-gather | bytes 655360 | tf_op jit(solution)/shard_map/all_gather | solution.py:128
  219.5 1.5 convolution_convert_fusion.8
  221.0 1.4 convolution_convert_fusion.9
  222.4 4.8 %collective-permute-start.13 = (bf16[256,256]{0,1:T(8,128)(2,1)S(1)}, bf16[256,256]{0,1:T(8,128)(2,1)S(1)}, u32[]{:S(2)}, u32[]{:S(2)}) collective-permute-start(bf16[256,256]{0,1:T(8,128)(2,1)S(1)} %pad_maximum_fusion.3), channel_id=1, source_target_pairs={{0,4},{4,8},{8,12},{12,16},{16,20},{20,24},{24,28},{28,32},{32,36}... | collective-permute-start | bytes 393224 | tf_op jit(solution)/shard_map/ppermute | solution.py:27
  227.2 3.8 %collective-permute-start.12 = (bf16[256,256]{0,1:T(8,128)(2,1)S(1)}, bf16[256,256]{0,1:T(8,128)(2,1)S(1)}, u32[]{:S(2)}, u32[]{:S(2)}) collective-permute-start(bf16[256,256]{0,1:T(8,128)(2,1)S(1)} %pad_maximum_fusion.3), channel_id=1, source_target_pairs={{0,8},{4,12},{8,16},{12,20},{16,24},{20,28},{24,32},{28,36},{32,40... | collective-permute-start | bytes 393224 | tf_op jit(solution)/shard_map/ppermute | solution.py:27
  231.0 1.7 convolution_convert_fusion.5
  233.0 1.3 collective-permute-start.15
  234.3 1.9 collective-permute-start.14
  236.3 4.9 %collective-permute-done.14 = bf16[256,256]{0,1:T(8,128)(2,1)S(1)} collective-permute-done((bf16[256,256]{0,1:T(8,128)(2,1)S(1)}, bf16[256,256]{0,1:T(8,128)(2,1)S(1)}, u32[]{:S(2)}, u32[]{:S(2)}) %collective-permute-start.14) | collective-permute-done | bytes 131104 | tf_op jit(solution)/shard_map/ppermute | solution.py:27
  244.6 3.7 %fusion.27 = bf16[8,128,2,64]{1,3,2,0:T(8,128)(2,1)S(1)} fusion(bf16[8,256,2,64]{1,3,2,0:T(8,128)(2,1)S(1)} %bitcast.198, f32[8,2,128]{2,1,0:T(2,128)S(1)} %fusion.141, bf16[8,256,2,64]{1,3,2,0:T(8,128)(2,1)S(1)} %bitcast.197, bf16[8,128,2,64]{3,2,1,0:T(2,128)(2,1)S(1)} %reshape.320), kind=kOutput, calls=%fused_computation.55 | convolution fusion | flops 136448256 | bytes 1581056 | tf_op jit(solution)/shard_map/bhrk,bkhd->brhd/dot_general | solution.py:57
  248.5 3.1 %convolution_convert_fusion = bf16[1024,1024]{1,0:T(8,128)(2,1)} fusion(bf16[16,8,8,128]{3,2,1,0:T(8,128)(2,1)S(1)} %bitcast.189, bf16[4,128,1024]{2,1,0:T(8,128)(2,1)} %param.18), kind=kOutput, calls=%fused_computation.21 | convolution fusion | flops 269484032 | bytes 2621440 | tf_op jit(solution)/shard_map/dot_general | solution.py:157
  251.7 47.5 %reduce-scatter.2.cloned.1.call-done = bf16[1024,256]{1,0:T(8,128)(2,1)} async-done(((bf16[1024,1024]{1,0:T(8,128)(2,1)}), bf16[1024,256]{1,0:T(8,128)(2,1)}) %reduce-scatter.2.cloned.1.call-update) | async-done | bytes 524304 | tf_op jit(solution)/shard_map/reduce_scatter | solution.py:158
  299.2 2.0 select_convert_fusion
  (155 shorter events, 30.3 us)
Async XLA Ops:
  10.0 5.2 %copy-start.5 = (f32[6,1024]{1,0:T(8,128)S(1)}, f32[6,1024]{1,0:T(8,128)}, u32[]{:S(2)}) copy-start(f32[6,1024]{1,0:T(8,128)} %param.19) | copy-start | bytes 73732
  10.0 5.2 %copy-start.3 = (bf16[256,256]{1,0:T(8,128)(2,1)S(1)}, bf16[256,256]{1,0:T(8,128)(2,1)}, u32[]{:S(2)}) copy-start(bf16[256,256]{1,0:T(8,128)(2,1)} %param.14) | copy-start | bytes 393220
  10.0 34.7 %copy-start.6 = (s32[1024]{0:T(1024)S(1)}, s32[1024]{0:T(1024)}, u32[]{:S(2)}) copy-start(s32[1024]{0:T(1024)} %param.23) | copy-start | bytes 12292
  10.0 34.7 %copy-start.7 = (s32[2,4]{1,0:T(2,128)S(1)}, s32[2,4]{1,0:T(2,128)}, u32[]{:S(2)}) copy-start(s32[2,4]{1,0:T(2,128)} %param.20) | copy-start | bytes 100
  10.0 36.8 %all-to-all-start = ((bf16[4,1024,256]{1,2,0:T(8,128)(2,1)}), bf16[4,1024,256]{1,2,0:T(8,128)(2,1)S(1)}, u32[]{:S(2)}, u32[]{:S(2)}) async-start(bf16[4,1024,256]{1,2,0:T(8,128)(2,1)} %stack.2), calls=%async_computation | async-start | bytes 4194304 | tf_op jit(solution)/shard_map/all_to_all | solution.py:108
  53.7 27.8 %collective-permute-start.1 = (bf16[1024,256]{0,1:T(8,128)(2,1)}, bf16[1024,256]{0,1:T(8,128)(2,1)}, u32[]{:S(2)}, u32[]{:S(2)}) collective-permute-start(bf16[1024,256]{0,1:T(8,128)(2,1)} %pad_maximum_fusion), channel_id=1, source_target_pairs={{0,4},{4,8},{8,12},{12,16},{16,20},{20,24},{24,28},{28,32},{32,36}... | collective-permute-start | bytes 1572872 | tf_op jit(solution)/shard_map/ppermute | solution.py:27
  62.8 17.7 %collective-permute-start = (bf16[1024,256]{0,1:T(8,128)(2,1)}, bf16[1024,256]{0,1:T(8,128)(2,1)}, u32[]{:S(2)}, u32[]{:S(2)}) collective-permute-start(bf16[1024,256]{0,1:T(8,128)(2,1)} %pad_maximum_fusion), channel_id=1, source_target_pairs={{0,8},{4,12},{8,16},{12,20},{16,24},{20,28},{24,32},{28,36},{32,40... | collective-permute-start | bytes 1572872 | tf_op jit(solution)/shard_map/ppermute | solution.py:27
  66.7 15.9 %collective-permute-start.2 = (bf16[1024,256]{0,1:T(8,128)(2,1)}, bf16[1024,256]{0,1:T(8,128)(2,1)}, u32[]{:S(2)}, u32[]{:S(2)}) collective-permute-start(bf16[1024,256]{0,1:T(8,128)(2,1)} %pad_maximum_fusion), channel_id=1, source_target_pairs={{4,0},{8,4},{12,8},{16,12},{20,16},{24,20},{28,24},{32,28},{36,32}... | collective-permute-start | bytes 1572872 | tf_op jit(solution)/shard_map/ppermute | solution.py:27
  68.8 16.1 %collective-permute-start.3 = (bf16[1024,256]{0,1:T(8,128)(2,1)}, bf16[1024,256]{0,1:T(8,128)(2,1)}, u32[]{:S(2)}, u32[]{:S(2)}) collective-permute-start(bf16[1024,256]{0,1:T(8,128)(2,1)} %pad_maximum_fusion), channel_id=1, source_target_pairs={{8,0},{12,4},{16,8},{20,12},{24,16},{28,20},{32,24},{36,28},{40,32... | collective-permute-start | bytes 1572872 | tf_op jit(solution)/shard_map/ppermute | solution.py:27
  92.0 1.2 copy-start.2
  93.1 4.8 %copy-start.8 = (s32[2,3]{1,0:T(2,128)S(1)}, s32[2,3]{1,0:T(2,128)}, u32[]{:S(2)}) copy-start(s32[2,3]{1,0:T(2,128)} %param.21) | copy-start | bytes 76
  93.1 4.9 %copy-start.9 = (s32[8,2]{0,1:T(2,128)S(1)}, s32[8,2]{0,1:T(2,128)}, u32[]{:S(2)}) copy-start(s32[8,2]{0,1:T(2,128)} %param.22) | copy-start | bytes 196
  94.4 10.4 %all-to-all-start.1 = ((bf16[4,256,256]{2,1,0:T(8,128)(2,1)}), bf16[4,256,256]{2,1,0:T(8,128)(2,1)S(1)}, u32[]{:S(2)}, u32[]{:S(2)}) async-start(bf16[4,256,256]{2,1,0:T(8,128)(2,1)} %bitcast.170), calls=%async_computation.1 | async-start | bytes 1048576 | tf_op jit(solution)/shard_map/all_to_all | solution.py:20
  119.2 18.2 %collective-permute-start.5 = (bf16[256,256]{0,1:T(8,128)(2,1)S(1)}, bf16[256,256]{0,1:T(8,128)(2,1)S(1)}, u32[]{:S(2)}, u32[]{:S(2)}) collective-permute-start(bf16[256,256]{0,1:T(8,128)(2,1)S(1)} %pad_maximum_fusion.1), channel_id=1, source_target_pairs={{0,4},{4,8},{8,12},{12,16},{16,20},{20,24},{24,28},{28,32},{32,36}... | collective-permute-start | bytes 393224 | tf_op jit(solution)/shard_map/ppermute | solution.py:27
  129.1 8.2 %collective-permute-start.4 = (bf16[256,256]{0,1:T(8,128)(2,1)S(1)}, bf16[256,256]{0,1:T(8,128)(2,1)S(1)}, u32[]{:S(2)}, u32[]{:S(2)}) collective-permute-start(bf16[256,256]{0,1:T(8,128)(2,1)S(1)} %pad_maximum_fusion.1), channel_id=1, source_target_pairs={{0,8},{4,12},{8,16},{12,20},{16,24},{20,28},{24,32},{28,36},{32,40... | collective-permute-start | bytes 393224 | tf_op jit(solution)/shard_map/ppermute | solution.py:27
  134.0 9.0 %collective-permute-start.7 = (bf16[256,256]{0,1:T(8,128)(2,1)S(1)}, bf16[256,256]{0,1:T(8,128)(2,1)S(1)}, u32[]{:S(2)}, u32[]{:S(2)}) collective-permute-start(bf16[256,256]{0,1:T(8,128)(2,1)S(1)} %pad_maximum_fusion.1), channel_id=1, source_target_pairs={{8,0},{12,4},{16,8},{20,12},{24,16},{28,20},{32,24},{36,28},{40,32... | collective-permute-start | bytes 393224 | tf_op jit(solution)/shard_map/ppermute | solution.py:27
  135.3 7.6 %collective-permute-start.6 = (bf16[256,256]{0,1:T(8,128)(2,1)S(1)}, bf16[256,256]{0,1:T(8,128)(2,1)S(1)}, u32[]{:S(2)}, u32[]{:S(2)}) collective-permute-start(bf16[256,256]{0,1:T(8,128)(2,1)S(1)} %pad_maximum_fusion.1), channel_id=1, source_target_pairs={{4,0},{8,4},{12,8},{16,12},{20,16},{24,20},{28,24},{32,28},{36,32}... | collective-permute-start | bytes 393224 | tf_op jit(solution)/shard_map/ppermute | solution.py:27
  170.4 16.8 %collective-permute-start.9 = (bf16[256,256]{0,1:T(8,128)(2,1)S(1)}, bf16[256,256]{0,1:T(8,128)(2,1)S(1)}, u32[]{:S(2)}, u32[]{:S(2)}) collective-permute-start(bf16[256,256]{0,1:T(8,128)(2,1)S(1)} %pad_maximum_fusion.2), channel_id=1, source_target_pairs={{0,4},{4,8},{8,12},{12,16},{16,20},{20,24},{24,28},{28,32},{32,36}... | collective-permute-start | bytes 393224 | tf_op jit(solution)/shard_map/ppermute | solution.py:27
  177.8 9.3 %collective-permute-start.8 = (bf16[256,256]{0,1:T(8,128)(2,1)S(1)}, bf16[256,256]{0,1:T(8,128)(2,1)S(1)}, u32[]{:S(2)}, u32[]{:S(2)}) collective-permute-start(bf16[256,256]{0,1:T(8,128)(2,1)S(1)} %pad_maximum_fusion.2), channel_id=1, source_target_pairs={{0,8},{4,12},{8,16},{12,20},{16,24},{20,28},{24,32},{28,36},{32,40... | collective-permute-start | bytes 393224 | tf_op jit(solution)/shard_map/ppermute | solution.py:27
  183.7 7.7 %collective-permute-start.11 = (bf16[256,256]{0,1:T(8,128)(2,1)S(1)}, bf16[256,256]{0,1:T(8,128)(2,1)S(1)}, u32[]{:S(2)}, u32[]{:S(2)}) collective-permute-start(bf16[256,256]{0,1:T(8,128)(2,1)S(1)} %pad_maximum_fusion.2), channel_id=1, source_target_pairs={{8,0},{12,4},{16,8},{20,12},{24,16},{28,20},{32,24},{36,28},{40,32... | collective-permute-start | bytes 393224 | tf_op jit(solution)/shard_map/ppermute | solution.py:27
  185.0 6.4 %collective-permute-start.10 = (bf16[256,256]{0,1:T(8,128)(2,1)S(1)}, bf16[256,256]{0,1:T(8,128)(2,1)S(1)}, u32[]{:S(2)}, u32[]{:S(2)}) collective-permute-start(bf16[256,256]{0,1:T(8,128)(2,1)S(1)} %pad_maximum_fusion.2), channel_id=1, source_target_pairs={{4,0},{8,4},{12,8},{16,12},{20,16},{24,20},{28,24},{32,28},{36,32}... | collective-permute-start | bytes 393224 | tf_op jit(solution)/shard_map/ppermute | solution.py:27
  195.8 12.0 %all-to-all-start.3 = ((bf16[4,256,256]{2,1,0:T(8,128)(2,1)}), bf16[4,256,256]{2,1,0:T(8,128)(2,1)S(1)}, u32[]{:S(2)}, u32[]{:S(2)}) async-start(bf16[4,256,256]{2,1,0:T(8,128)(2,1)} %bitcast.166), calls=%async_computation.3 | async-start | bytes 1048576 | tf_op jit(solution)/shard_map/all_to_all | solution.py:20
  199.3 100.0 %reduce-scatter.2.cloned.1.call-start = ((), (), s32[]{:S(2)}) async-start(), calls=%async_computation.5 | async-start | bytes 2621440 | tf_op jit(solution)/shard_map/reduce_scatter | solution.py:158
  207.9 14.5 %copy-start.4 = (bf16[256,256]{1,0:T(8,128)(2,1)}, bf16[256,256]{1,0:T(8,128)(2,1)S(1)}, u32[]{:S(2)}) copy-start(bf16[256,256]{1,0:T(8,128)(2,1)S(1)} %add_convert_fusion) | copy-start | bytes 393220
  219.0 12.0 %copy-start = (bf16[4,1024,256]{1,2,0:T(8,128)(2,1)S(1)}, bf16[4,1024,256]{1,2,0:T(8,128)(2,1)}, u32[]{:S(2)}) copy-start(bf16[4,1024,256]{1,2,0:T(8,128)(2,1)} %get-tuple-element.11) | copy-start | bytes 6291460
  222.4 13.9 %collective-permute-start.13 = (bf16[256,256]{0,1:T(8,128)(2,1)S(1)}, bf16[256,256]{0,1:T(8,128)(2,1)S(1)}, u32[]{:S(2)}, u32[]{:S(2)}) collective-permute-start(bf16[256,256]{0,1:T(8,128)(2,1)S(1)} %pad_maximum_fusion.3), channel_id=1, source_target_pairs={{0,4},{4,8},{8,12},{12,16},{16,20},{20,24},{24,28},{28,32},{32,36}... | collective-permute-start | bytes 393224 | tf_op jit(solution)/shard_map/ppermute | solution.py:27
  227.2 9.0 %collective-permute-start.12 = (bf16[256,256]{0,1:T(8,128)(2,1)S(1)}, bf16[256,256]{0,1:T(8,128)(2,1)S(1)}, u32[]{:S(2)}, u32[]{:S(2)}) collective-permute-start(bf16[256,256]{0,1:T(8,128)(2,1)S(1)} %pad_maximum_fusion.3), channel_id=1, source_target_pairs={{0,8},{4,12},{8,16},{12,20},{16,24},{20,28},{24,32},{28,36},{32,40... | collective-permute-start | bytes 393224 | tf_op jit(solution)/shard_map/ppermute | solution.py:27
  233.0 9.0 %collective-permute-start.15 = (bf16[256,256]{0,1:T(8,128)(2,1)S(1)}, bf16[256,256]{0,1:T(8,128)(2,1)S(1)}, u32[]{:S(2)}, u32[]{:S(2)}) collective-permute-start(bf16[256,256]{0,1:T(8,128)(2,1)S(1)} %pad_maximum_fusion.3), channel_id=1, source_target_pairs={{8,0},{12,4},{16,8},{20,12},{24,16},{28,20},{32,24},{36,28},{40,32... | collective-permute-start | bytes 393224 | tf_op jit(solution)/shard_map/ppermute | solution.py:27
  234.3 6.9 %collective-permute-start.14 = (bf16[256,256]{0,1:T(8,128)(2,1)S(1)}, bf16[256,256]{0,1:T(8,128)(2,1)S(1)}, u32[]{:S(2)}, u32[]{:S(2)}) collective-permute-start(bf16[256,256]{0,1:T(8,128)(2,1)S(1)} %pad_maximum_fusion.3), channel_id=1, source_target_pairs={{4,0},{8,4},{12,8},{16,12},{20,16},{24,20},{28,24},{32,28},{36,32}... | collective-permute-start | bytes 393224 | tf_op jit(solution)/shard_map/ppermute | solution.py:27
  248.5 50.8 %copy-start.1 = (bf16[1024,256]{1,0:T(8,128)(2,1)S(1)}, bf16[1024,256]{1,0:T(8,128)(2,1)}, u32[]{:S(2)}) copy-start(bf16[1024,256]{1,0:T(8,128)(2,1)} %param.13) | copy-start | bytes 1572868
Sparse Core Ops, SparseCore 0:
  251.7 47.4 reduce-scatter.1
